TPU v7x, 256 devices: a whole 4x4x8 slice. The times are simulated.
256 devices in a mesh: chan: 4 (over x), sym: 4 (over z_hi), sub: 16 (over y, z_lo, core).
Axes of the slice: x: 4, y: 4, z: 8 (z_hi: 4, z_lo: 2; z = z_hi * 2 + z_lo), core: 2. Of those that a mesh axis runs over, the one named last changes fastest.
Arguments:
- samples: float32 [2, 64, 24, 9216], P(None, ('chan', 'sub'), 'sym'), parts along dimension 1, may hold values from -16 to 16
- constellation_index: int32 [96, 4096], P(('chan', 'sym'), 'sub'), parts along dimension 0, may hold values from 0 to 63, as said below
- pilot_offsets: int32 [24], P('sym'), may hold values from 0 to 11
- cp_offset: int32 [96], P(('chan', 'sym')), parts along dimension 0, may hold values from 0 to 1024, as said below
Outputs:
- caf: float32 [2, 64, 24, 1024], P(None, 'chan', 'sym', 'sub'), parts along dimension 1
There are 4 independent parts, one for each index of `chan`. A program takes and returns all parts, laid end to end along the dimension named above; an argument that names none is the same for every part. Nothing has to cross between parts.
Inputs may be any that keep to these rules, and one draw needn't show every extreme that they name: Symbol m's scattered pilots sit on the active subcarriers k with k mod 12 == pilot_offsets[m]. The transform window of symbol m is samples cp_offset[m] to cp_offset[m] + 64 * 128 - 1 of its record. `constellation_index`: the index's low three bits give the in-phase level, the high three the quadrature level.
All inputs are finite; a program needn't handle non-finite values.
Results may differ from a plain program's by a relative error of at most 0.0003.
Values may be sent and summed in bfloat16 or wider, within the bound.
A program may use at most 64 MiB of HBM per device.

v0:
```python
import functools
import math

import jax
import jax.numpy as jnp
import ml_dtypes
import numpy as np
from jax import lax
from jax.experimental import pallas as pl
from jax.experimental.pallas import tpu as pltpu
from jax.sharding import PartitionSpec as P

MESH = pl.DeviceIdType.MESH
BF16 = jnp.bfloat16
F32 = jnp.float32

LENGTH = 8192
TONES = 4096
LOWEST = 2048
RADIX = 32
LANES = 128
GUARD = 1024
HALFSPAN = 48
PSP = 12
SYM = 4
SUB = 16
MS = 6
SYMBOLS = 24
SHIFTS = (-2, -1, 0, 1, 2)


def halves(matrix):
    high = matrix.astype(ml_dtypes.bfloat16)
    low = (matrix - high.astype(np.float64)).astype(ml_dtypes.bfloat16)
    return high, low


def tables():
    p = np.arange(RADIX)
    turn = 2.0 * np.pi
    c = np.cos(turn * np.outer(p, p) / RADIX)
    s = np.sin(turn * np.outer(p, p) / RADIX)
    high, low = halves(np.block([[c, s], [-s, c]]))
    first = np.concatenate([high, low, high], axis=1)
    b = np.arange(256)
    angle = turn * np.outer(p, b) / LENGTH
    twist = np.stack([np.cos(angle), np.sin(angle)]).astype(np.float32)
    j = LOWEST // RADIX + np.arange(LANES)
    angle = turn * (np.outer(b, j) % 256) / 256
    c, s = np.cos(angle), np.sin(angle)
    second = np.stack(halves(np.block([[c, -s], [s, c]]) / math.sqrt(LENGTH)))
    rows = []
    for shift in SHIFTS:
        gap = RADIX * shift + p[None, :] - p[:, None]
        rows.append(np.maximum(HALFSPAN + 1 - np.abs(gap), 0))
    taper = np.concatenate(rows, axis=0)
    taper = np.concatenate([taper, taper], axis=1).astype(ml_dtypes.bfloat16)
    v = np.arange(LANES)
    angle = turn * (np.outer(v, v) % LANES) / LANES
    c, s = np.cos(angle), np.sin(angle)
    third = np.stack(halves(np.block([[c, s], [-s, c]]) / math.sqrt(TONES * SYMBOLS)))
    angle = turn * np.outer(p, v) / TONES
    twirl = np.stack([np.cos(angle), np.sin(angle)]).astype(np.float32)
    u = np.arange(GUARD // LANES)
    angle = turn * (np.outer(u, p) % RADIX) / RADIX
    c, s = np.cos(angle), np.sin(angle)
    high, low = halves(np.block([[c, -s], [s, c]]))
    fourth = np.concatenate([high, low, high], axis=1)
    spread = np.zeros((4, RADIX, LANES), ml_dtypes.bfloat16)
    for g in range(4):
        spread[g, p, 4 * p + g] = 1
    doppler = np.zeros((SYM, 16, 64), np.float64)
    for block in range(SYM):
        for f in range(MS):
            for source in range(SYM):
                for m in range(MS):
                    angle = turn * (((MS * source + m) * (MS * block + f)) % SYMBOLS) / SYMBOLS
                    doppler[block, f, 8 * source + m] = np.cos(angle)
                    doppler[block, f, 32 + 8 * source + m] = np.sin(angle)
    high, low = halves(doppler)
    doppler = np.concatenate([high, low, high], axis=2)
    return first, twist, second, taper, third, twirl, fourth, spread, doppler


def dot(a, b):
    return jnp.dot(a, b, preferred_element_type=F32)


def parted(value):
    high = value.astype(BF16)
    low = (value - high.astype(F32)).astype(BF16)
    return high, low


def kernel(
    cp_ref,
    pilot_ref,
    x_hbm,
    index_ref,
    first_ref,
    twist_ref,
    second_ref,
    taper_ref,
    third_ref,
    twirl_ref,
    fourth_ref,
    spread_ref,
    doppler_ref,
    out_ref,
    x_ref,
    y_ref,
    zh_ref,
    zl_ref,
    itmp_ref,
    isend_ref,
    igath_ref,
    ig_ref,
    send_ref,
    recv_ref,
    x_sem,
    isend_sem,
    irecv_sem,
    send_sem,
    recv_sem,
    ready_sem,
):
    sym = lax.axis_index("sym")
    sub = lax.axis_index("sub")
    barrier = pltpu.get_barrier_semaphore()

    load = pltpu.make_async_copy(x_hbm.at[:, 0], x_ref, x_sem)
    load.start()

    for d in range(1, SUB):
        pl.semaphore_signal(
            barrier, inc=1, device_id={"sub": lax.rem(sub + d, SUB)}, device_id_type=MESH
        )
    for d in range(1, SYM):
        pl.semaphore_signal(
            barrier, inc=1, device_id={"sym": lax.rem(sym + d, SYM)}, device_id_type=MESH
        )

    itmp_ref[...] = jnp.zeros_like(itmp_ref)
    index = index_ref[...].astype(F32)
    itmp_ref[0:MS, :] = index[:, :LANES]
    itmp_ref[8 : 8 + MS, :] = index[:, LANES:]
    isend_ref[...] = itmp_ref[...].astype(BF16)
    send_ref[...] = jnp.zeros_like(send_ref)

    lane = lax.broadcasted_iota(jnp.int32, (RADIX, LANES), 1)
    row = lax.broadcasted_iota(jnp.int32, (RADIX, LANES), 0)
    start_lanes = jnp.zeros((RADIX, LANES), jnp.int32)
    row8 = lax.broadcasted_iota(jnp.int32, (8, LANES), 0)
    lane8 = lax.broadcasted_iota(jnp.int32, (8, LANES), 1)
    start_rows = jnp.zeros((8, LANES), jnp.int32)
    for m in range(MS):
        start_lanes = jnp.where(lane == m, cp_ref[m], start_lanes)
        start_rows = jnp.where(row8 == m, cp_ref[m], start_rows)
    step = 2.0 * math.pi / LENGTH
    angle = ((start_lanes * row) & (LENGTH - 1)).astype(F32) * step
    row_cos, row_sin = jnp.cos(angle), jnp.sin(angle)
    angle = ((start_rows * (LOWEST + RADIX * lane8)) & (LENGTH - 1)).astype(F32) * step
    lane_cos, lane_sin = jnp.cos(angle), jnp.sin(angle)
    residue = lax.rem(RADIX * lane + row, PSP)

    load.wait()
    lane6 = lax.broadcasted_iota(jnp.int32, (MS, LANES), 1)
    starts = start_rows[0:MS]
    for part in range(2):
        for t in range(LENGTH // LANES):
            value = x_ref[part, :, pl.ds(t * LANES, LANES)]
            if t * LANES < GUARD:
                later = x_ref[part, :, pl.ds(LENGTH + t * LANES, LANES)]
                value = jnp.where(lane6 + t * LANES >= starts, value, later)
            y_ref[t % 2, pl.ds(part * RADIX + t // 2, MS, stride=64), :] = value

    twist_cos, twist_sin = twist_ref[0], twist_ref[1]
    for m in range(MS):
        value = jnp.concatenate(
            [y_ref[0, pl.ds(64 * m, 64), :], y_ref[1, pl.ds(64 * m, 64), :]], axis=1
        )
        high, low = parted(value)
        y = dot(first_ref[...], jnp.concatenate([high, high, low], axis=0))
        re, im = y[:RADIX], y[RADIX:]
        z = jnp.concatenate(
            [re * twist_cos + im * twist_sin, im * twist_cos - re * twist_sin], axis=1
        )
        high, low = parted(z)
        zh_ref[pl.ds(RADIX * m, RADIX), :] = high
        zl_ref[pl.ds(RADIX * m, RADIX), :] = low

    pl.semaphore_wait(barrier, SUB + SYM - 2)
    mine = pl.ds(pl.multiple_of(16 * sub, 16), 16)
    for d in range(1, SUB):
        pltpu.make_async_remote_copy(
            src_ref=isend_ref,
            dst_ref=igath_ref.at[mine],
            send_sem=isend_sem,
            recv_sem=irecv_sem,
            device_id={"sub": lax.rem(sub + d, SUB)},
            device_id_type=MESH,
        ).start()
    for d in range(1, SYM):
        pl.semaphore_signal(
            ready_sem, inc=1, device_id={"sym": lax.rem(sym + d, SYM)}, device_id_type=MESH
        )
    igath_ref[mine, :] = isend_ref[...]

    zh = zh_ref[...]
    spectra = dot(zh, second_ref[0]) + dot(zl_ref[...], second_ref[0]) + dot(zh, second_ref[1])

    all_index = igath_ref.at[pl.ds(0, 16 * (SUB - 1))]
    pltpu.make_async_remote_copy(
        src_ref=all_index,
        dst_ref=all_index,
        send_sem=isend_sem,
        recv_sem=irecv_sem,
        device_id={"sub": lax.rem(sub + 1, SUB)},
        device_id_type=MESH,
    ).wait()
    ig_ref[...] = igath_ref[...].astype(F32)

    natural = [jnp.transpose(ig_ref[pl.ds(m, RADIX, stride=8), :]) for m in range(MS)]
    natural = [value.astype(BF16) for value in natural]
    index = sum(
        dot(
            jnp.concatenate([value[RADIX * g : RADIX * (g + 1)] for value in natural], axis=0),
            spread_ref[g],
        )
        for g in range(4)
    )

    high_rows, low_rows = [], []
    for m in range(MS):
        rows = slice(RADIX * m, RADIX * (m + 1))
        quadrature = jnp.floor(index[rows] * 0.125)
        level_re = 2.0 * (index[rows] - 8.0 * quadrature) - 7.0
        level_im = 2.0 * quadrature - 7.0
        factor = math.sqrt(42.0) / (level_re * level_re + level_im * level_im)
        lc = lane_cos[m : m + 1, :]
        ls = lane_sin[m : m + 1, :]
        rc = jnp.broadcast_to(row_cos[:, m : m + 1], (RADIX, LANES))
        rs = jnp.broadcast_to(row_sin[:, m : m + 1], (RADIX, LANES))
        phase_re = (lc * rc - ls * rs) * factor
        phase_im = (lc * rs + ls * rc) * factor
        gain_re = phase_re * level_re + phase_im * level_im
        gain_im = phase_im * level_re - phase_re * level_im
        re, im = spectra[rows, :LANES], spectra[rows, LANES:]
        ratio_re = re * gain_re - im * gain_im
        ratio_im = re * gain_im + im * gain_re
        ratio = jnp.concatenate([ratio_re, ratio_im], axis=1)
        pilot = (residue == pilot_ref[m]).astype(F32)
        high, low = parted(ratio * jnp.concatenate([pilot, pilot], axis=1))
        right = jnp.concatenate(
            [
                jnp.concatenate([high, pilot.astype(BF16)], axis=1),
                jnp.concatenate([low, jnp.zeros((RADIX, LANES), BF16)], axis=1),
            ],
            axis=0,
        )
        tapered = dot(taper_ref[...], right)
        sums = []
        for part in range(3):
            total = None
            for i, shift in enumerate(SHIFTS):
                term = tapered[RADIX * i : RADIX * (i + 1), LANES * part : LANES * (part + 1)]
                if shift:
                    term = pltpu.roll(term, (-shift) % LANES, 1)
                    inside = lane < LANES - shift if shift > 0 else lane >= -shift
                    term = jnp.where(inside, term, 0.0)
                total = term if total is None else total + term
            sums.append(total)
        inverse = 1.0 / sums[2]
        cleaned = jnp.concatenate(
            [ratio_re - sums[0] * inverse, ratio_im - sums[1] * inverse], axis=1
        )
        high, low = parted(cleaned)
        high_rows.append(high)
        low_rows.append(low)
    high = jnp.concatenate(high_rows, axis=0)
    low = jnp.concatenate(low_rows, axis=0)
    folded = dot(high, third_ref[0]) + dot(low, third_ref[0]) + dot(high, third_ref[1])

    twirl_cos, twirl_sin = twirl_ref[0], twirl_ref[1]
    columns = []
    for m in range(MS):
        rows = slice(RADIX * m, RADIX * (m + 1))
        re, im = folded[rows, :LANES], folded[rows, LANES:]
        value = jnp.concatenate(
            [re * twirl_cos - im * twirl_sin, re * twirl_sin + im * twirl_cos], axis=0
        )
        high, low = parted(value)
        columns.append(jnp.concatenate([high, high, low], axis=0))
    profile = dot(fourth_ref[...], jnp.concatenate(columns, axis=1))
    for m in range(MS):
        re = profile[0:8, LANES * m : LANES * (m + 1)]
        im = profile[8:16, LANES * m : LANES * (m + 1)]
        send_ref[0, pl.ds(m, 8, stride=8), :] = jnp.where(lane8 < 64, re, pltpu.roll(im, 64, 1))
        send_ref[1, pl.ds(m, 8, stride=8), :] = jnp.where(lane8 < 64, pltpu.roll(re, 64, 1), im)

    pl.semaphore_wait(ready_sem, SYM - 1)
    slot = pl.ds(pl.multiple_of(8 * (SYM * sub + sym), 8), 8)

    def block(to_sub):
        return send_ref.at[lax.rem(to_sub, 2), pl.ds(pl.multiple_of(8 * (to_sub // 2), 8), 8)]

    for e in (2, 1, 3, 0):
        for d in range(SUB):
            if e == 0 and d == 0:
                continue
            to_sub = lax.rem(sub + d, SUB)
            pltpu.make_async_remote_copy(
                src_ref=block(to_sub),
                dst_ref=recv_ref.at[slot],
                send_sem=send_sem,
                recv_sem=recv_sem,
                device_id={"sym": lax.rem(sym + e, SYM), "sub": to_sub},
                device_id_type=MESH,
            ).start()
    recv_ref[slot, :] = send_ref[lax.rem(sub, 2), pl.ds(pl.multiple_of(8 * (sub // 2), 8), 8), :]

    everything = recv_ref.at[pl.ds(0, 8 * (SYM * SUB - 1))]
    pltpu.make_async_remote_copy(
        src_ref=everything,
        dst_ref=everything,
        send_sem=send_sem,
        recv_sem=recv_sem,
        device_id={"sub": lax.rem(sub + 1, SUB)},
        device_id_type=MESH,
    ).wait()

    columns = []
    for c in range(SUB):
        value = recv_ref[pl.ds(32 * c, 32), :]
        turned = pltpu.roll(value, 64, 1)
        turned = jnp.where(lane < 64, turned, -turned)
        high, low = parted(jnp.concatenate([value, turned], axis=0))
        columns.append(jnp.concatenate([high, high, low], axis=0))
    result = dot(doppler_ref[sym], jnp.concatenate(columns, axis=1))
    for c in range(SUB):
        value = result[0:8, LANES * c : LANES * (c + 1)]
        out_ref[0, c, :, :] = value[0:MS, 0:64]
        out_ref[1, c, :, :] = pltpu.roll(value, 64, 1)[0:MS, 0:64]


def body(samples, constellation_index, pilot_offsets, cp_offset):
    consts = [jnp.asarray(table) for table in tables()]
    smem = pl.BlockSpec(memory_space=pltpu.SMEM)
    vmem = pl.BlockSpec(memory_space=pltpu.VMEM)
    hbm = pl.BlockSpec(memory_space=pl.ANY)
    return pl.pallas_call(
        kernel,
        out_shape=jax.ShapeDtypeStruct((2, SUB, MS, GUARD // SUB), F32),
        in_specs=[smem, smem, hbm] + [vmem] * (1 + len(consts)),
        out_specs=vmem,
        scratch_shapes=[
            pltpu.VMEM((2, MS, LENGTH + GUARD), F32),
            pltpu.VMEM((2, 64 * MS, LANES), F32),
            pltpu.VMEM((RADIX * MS, 512), BF16),
            pltpu.VMEM((RADIX * MS, 512), BF16),
            pltpu.VMEM((16, LANES), F32),
            pltpu.VMEM((16, LANES), BF16),
            pltpu.VMEM((16 * SUB, LANES), BF16),
            pltpu.VMEM((16 * SUB, LANES), F32),
            pltpu.VMEM((2, 64, LANES), F32),
            pltpu.VMEM((8 * SYM * SUB, LANES), F32),
            pltpu.SemaphoreType.DMA,
            pltpu.SemaphoreType.DMA,
            pltpu.SemaphoreType.DMA,
            pltpu.SemaphoreType.DMA,
            pltpu.SemaphoreType.DMA,
            pltpu.SemaphoreType.REGULAR,
        ],
        compiler_params=pltpu.CompilerParams(collective_id=0, has_side_effects=True),
    )(cp_offset, pilot_offsets, samples, constellation_index, *consts)


def solution(mesh):
    return jax.shard_map(
        body,
        mesh=mesh,
        in_specs=(
            P(None, ("chan", "sub"), "sym", None),
            P(("chan", "sym"), "sub"),
            P("sym"),
            P(("chan", "sym")),
        ),
        out_specs=P(None, "chan", "sym", "sub"),
        check_vma=False,
    )
```

profile of v0, /device:TPU:1, one launch (start us, length us, event | category | flops | bytes accessed | tf_op | source)
XLA Modules:
  0.0 29.4 jit_solution(13540144336881454952)
XLA Ops:
  0.0 1.9 %copy.14.x_hbm = f32[2,1,6,9216]{3,2,1,0:T(8,128)} copy(f32[2,1,6,9216]{3,1,2,0:T(1,128)} %param.13) | data formatting | bytes 884736 | tf_op args[0]
  1.9 25.9 %shard_map.127 = f32[2,16,6,64]{3,2,1,0:T(8,128)} custom-call(s32[6]{0:T(128)} %cp_ref.1, s32[6]{0:T(128)} %pilot_ref.1, f32[2,1,6,9216]{3,2,1,0:T(8,128)} %copy.14.x_hbm, s32[6,256]{1,0:T(8,128)} %index_ref.1, bf16[64,192]{1,0:T(8,128)(2,1)} %constant.18.clone.first_ref, f32[2,32,256]{2,1,0:T(8,128)} %constant.19.clone.twist_ref, ...), custom_call_target="tpu_custom_call" | custom-call | tf_op jit(solution)/shard_map/pallas_call | solution.py:351
  27.9 1.6 %copy.15 = f32[2,16,6,64]{3,1,2,0:T(8,128)} copy(f32[2,16,6,64]{3,2,1,0:T(8,128)} %shard_map.127) | data formatting | bytes 98304 | tf_op jit(solution)/shard_map/pallas_call | solution.py:351
where the time goes:
time: 29.6 us; the launch traced here: 29.4 us
  Pallas kernels  25.9 us (88%)
  local copies, waits for them, and re-layouts  3.5 us (12%)
    pallas_call x1, Pallas kernels, body(): pl.pallas_call(kernel, out_shape=jax.ShapeDtypeStruct((2, SUB, MS, GUARD...  25.9 us
    unnamed x1, local copies, waits for them, and re-layouts  1.93 us
    pallas_call x1, local copies, waits for them, and re-layouts, body(): pl.pallas_call(kernel, out_shape=jax.ShapeDtypeStruct((2, SUB, MS, GUARD...  1.57 us

commit v1 on v0

--- a/solution.py
+++ b/solution.py
@@ -68,17 +68,15 @@
     fourth = np.concatenate([high, low, high], axis=1)
     spread = np.zeros((4, RADIX, LANES), ml_dtypes.bfloat16)
     for g in range(4):
-        spread[g, p, 4 * p + g] = 1
-    doppler = np.zeros((SYM, 16, 64), np.float64)
+        for half in range(2):
+            for owner in range(SUB):
+                spread[g, SUB * half + owner, 4 * (2 * owner + half) + g] = 1
+    f, m = np.arange(MS), np.arange(SYMBOLS)
+    doppler = np.zeros((SYM, 2, MS, SYMBOLS), np.float32)
     for block in range(SYM):
-        for f in range(MS):
-            for source in range(SYM):
-                for m in range(MS):
-                    angle = turn * (((MS * source + m) * (MS * block + f)) % SYMBOLS) / SYMBOLS
-                    doppler[block, f, 8 * source + m] = np.cos(angle)
-                    doppler[block, f, 32 + 8 * source + m] = np.sin(angle)
-    high, low = halves(doppler)
-    doppler = np.concatenate([high, low, high], axis=2)
+        angle = turn * (np.outer(MS * block + f, m) % SYMBOLS) / SYMBOLS
+        doppler[block] = np.cos(angle), np.sin(angle)
+    doppler = doppler.reshape(SYM, 2 * MS * SYMBOLS)
     return first, twist, second, taper, third, twirl, fourth, spread, doppler
 
 
@@ -92,10 +90,27 @@
     return high, low
 
 
+RECORD = 72
+
+
 def kernel(
+    cp_hbm,
+    pilot_hbm,
+    x_hbm,
+    index_hbm,
+    first_hbm,
+    twist_hbm,
+    second_hbm,
+    taper_hbm,
+    third_hbm,
+    twirl_hbm,
+    fourth_hbm,
+    spread_hbm,
+    doppler_hbm,
+    out_ref,
     cp_ref,
     pilot_ref,
-    x_hbm,
+    x_ref,
     index_ref,
     first_ref,
     twist_ref,
@@ -106,52 +121,84 @@
     fourth_ref,
     spread_ref,
     doppler_ref,
-    out_ref,
-    x_ref,
-    y_ref,
     zh_ref,
     zl_ref,
-    itmp_ref,
     isend_ref,
     igath_ref,
     ig_ref,
+    stage_ref,
     send_ref,
     recv_ref,
-    x_sem,
+    got_ref,
+    load_sem,
     isend_sem,
     irecv_sem,
     send_sem,
     recv_sem,
-    ready_sem,
+    near_sem,
+    far_sem,
 ):
     sym = lax.axis_index("sym")
     sub = lax.axis_index("sub")
     barrier = pltpu.get_barrier_semaphore()
-
-    load = pltpu.make_async_copy(x_hbm.at[:, 0], x_ref, x_sem)
-    load.start()
+    before, after = lax.rem(sym + SYM - 1, SYM), lax.rem(sym + 1, SYM)
 
     for d in range(1, SUB):
         pl.semaphore_signal(
             barrier, inc=1, device_id={"sub": lax.rem(sub + d, SUB)}, device_id_type=MESH
         )
-    for d in range(1, SYM):
-        pl.semaphore_signal(
-            barrier, inc=1, device_id={"sym": lax.rem(sym + d, SYM)}, device_id_type=MESH
-        )
-
-    itmp_ref[...] = jnp.zeros_like(itmp_ref)
-    index = index_ref[...].astype(F32)
-    itmp_ref[0:MS, :] = index[:, :LANES]
-    itmp_ref[8 : 8 + MS, :] = index[:, LANES:]
-    isend_ref[...] = itmp_ref[...].astype(BF16)
-    send_ref[...] = jnp.zeros_like(send_ref)
+    for to in (before, after):
+        pl.semaphore_signal(barrier, inc=1, device_id={"sym": to}, device_id_type=MESH)
+
+    loads = [
+        pltpu.make_async_copy(source, target, load_sem.at[i])
+        for i, (source, target) in enumerate(
+            (
+                (index_hbm, index_ref),
+                (cp_hbm, cp_ref),
+                (x_hbm, x_ref),
+                (first_hbm, first_ref),
+                (twist_hbm, twist_ref),
+                (second_hbm, second_ref),
+                (pilot_hbm, pilot_ref),
+                (spread_hbm, spread_ref),
+                (taper_hbm, taper_ref),
+                (third_hbm, third_ref),
+                (twirl_hbm, twirl_ref),
+                (fourth_hbm, fourth_ref),
+                (doppler_hbm.at[pl.ds(sym, 1)], doppler_ref),
+            )
+        )
+    ]
+    for load in loads:
+        load.start()
 
     lane = lax.broadcasted_iota(jnp.int32, (RADIX, LANES), 1)
     row = lax.broadcasted_iota(jnp.int32, (RADIX, LANES), 0)
-    start_lanes = jnp.zeros((RADIX, LANES), jnp.int32)
     row8 = lax.broadcasted_iota(jnp.int32, (8, LANES), 0)
     lane8 = lax.broadcasted_iota(jnp.int32, (8, LANES), 1)
+    residue = lax.rem(RADIX * lane + row, PSP)
+
+    loads[0].wait()
+    index = index_ref[...].astype(F32)
+    isend_ref[...] = jnp.concatenate([index[:, :LANES], index[:, LANES:]], axis=0).astype(BF16)
+
+    pl.semaphore_wait(barrier, SUB + 1)
+    for d in (8, 9, 10, 11, 7, 6, 5, 4, 12, 13, 14, 15, 3, 2, 1):
+        pltpu.make_async_remote_copy(
+            src_ref=isend_ref,
+            dst_ref=igath_ref.at[sub],
+            send_sem=isend_sem,
+            recv_sem=irecv_sem,
+            device_id={"sub": lax.rem(sub + d, SUB)},
+            device_id_type=MESH,
+        ).start()
+    for to in (before, after):
+        pl.semaphore_signal(near_sem, inc=1, device_id={"sym": to}, device_id_type=MESH)
+    igath_ref[sub] = isend_ref[...]
+
+    loads[1].wait()
+    start_lanes = jnp.zeros((RADIX, LANES), jnp.int32)
     start_rows = jnp.zeros((8, LANES), jnp.int32)
     for m in range(MS):
         start_lanes = jnp.where(lane == m, cp_ref[m], start_lanes)
@@ -161,25 +208,24 @@
     row_cos, row_sin = jnp.cos(angle), jnp.sin(angle)
     angle = ((start_rows * (LOWEST + RADIX * lane8)) & (LENGTH - 1)).astype(F32) * step
     lane_cos, lane_sin = jnp.cos(angle), jnp.sin(angle)
-    residue = lax.rem(RADIX * lane + row, PSP)
-
-    load.wait()
-    lane6 = lax.broadcasted_iota(jnp.int32, (MS, LANES), 1)
-    starts = start_rows[0:MS]
-    for part in range(2):
-        for t in range(LENGTH // LANES):
-            value = x_ref[part, :, pl.ds(t * LANES, LANES)]
-            if t * LANES < GUARD:
-                later = x_ref[part, :, pl.ds(LENGTH + t * LANES, LANES)]
-                value = jnp.where(lane6 + t * LANES >= starts, value, later)
-            y_ref[t % 2, pl.ds(part * RADIX + t // 2, MS, stride=64), :] = value
-
+
+    for i in (2, 3, 4):
+        loads[i].wait()
+    place = LANES * row8 + lane8
     twist_cos, twist_sin = twist_ref[0], twist_ref[1]
     for m in range(MS):
-        value = jnp.concatenate(
-            [y_ref[0, pl.ds(64 * m, 64), :], y_ref[1, pl.ds(64 * m, 64), :]], axis=1
-        )
-        high, low = parted(value)
+        pieces = []
+        for part in range(2):
+            base = RECORD * (MS * part + m)
+            x_ref[pl.ds(base, 8), :] = jnp.where(
+                place >= cp_ref[m], x_ref[pl.ds(base, 8), :], x_ref[pl.ds(base + 64, 8), :]
+            )
+            pieces.append(
+                jnp.concatenate(
+                    [x_ref[pl.ds(base + i, RADIX, stride=2), :] for i in range(2)], axis=1
+                )
+            )
+        high, low = parted(jnp.concatenate(pieces, axis=0))
         y = dot(first_ref[...], jnp.concatenate([high, high, low], axis=0))
         re, im = y[:RADIX], y[RADIX:]
         z = jnp.concatenate(
@@ -188,40 +234,34 @@
         high, low = parted(z)
         zh_ref[pl.ds(RADIX * m, RADIX), :] = high
         zl_ref[pl.ds(RADIX * m, RADIX), :] = low
-
-    pl.semaphore_wait(barrier, SUB + SYM - 2)
-    mine = pl.ds(pl.multiple_of(16 * sub, 16), 16)
-    for d in range(1, SUB):
-        pltpu.make_async_remote_copy(
-            src_ref=isend_ref,
-            dst_ref=igath_ref.at[mine],
-            send_sem=isend_sem,
-            recv_sem=irecv_sem,
-            device_id={"sub": lax.rem(sub + d, SUB)},
-            device_id_type=MESH,
-        ).start()
-    for d in range(1, SYM):
-        pl.semaphore_signal(
-            ready_sem, inc=1, device_id={"sym": lax.rem(sym + d, SYM)}, device_id_type=MESH
-        )
-    igath_ref[mine, :] = isend_ref[...]
-
+    loads[5].wait()
     zh = zh_ref[...]
     spectra = dot(zh, second_ref[0]) + dot(zl_ref[...], second_ref[0]) + dot(zh, second_ref[1])
 
-    all_index = igath_ref.at[pl.ds(0, 16 * (SUB - 1))]
-    pltpu.make_async_remote_copy(
+    for i in range(6, 13):
+        loads[i].wait()
+    pl.semaphore_wait(near_sem, 2)
+    pl.semaphore_signal(far_sem, inc=1, device_id={"sym": before}, device_id_type=MESH)
+
+    all_index = igath_ref.at[pl.ds(0, SUB - 1)]
+    index_copies = pltpu.make_async_remote_copy(
         src_ref=all_index,
         dst_ref=all_index,
         send_sem=isend_sem,
         recv_sem=irecv_sem,
         device_id={"sub": lax.rem(sub + 1, SUB)},
         device_id_type=MESH,
-    ).wait()
-    ig_ref[...] = igath_ref[...].astype(F32)
-
-    natural = [jnp.transpose(ig_ref[pl.ds(m, RADIX, stride=8), :]) for m in range(MS)]
-    natural = [value.astype(BF16) for value in natural]
+    )
+    index_copies.wait_recv()
+    for owner in range(SUB):
+        ig_ref[pl.ds(16 * owner, 2 * MS), :] = igath_ref[owner].astype(F32)
+
+    natural = []
+    for m in range(MS):
+        value = jnp.concatenate(
+            [ig_ref[pl.ds(MS * half + m, SUB, stride=16), :] for half in range(2)], axis=0
+        )
+        natural.append(jnp.transpose(value).astype(BF16))
     index = sum(
         dot(
             jnp.concatenate([value[RADIX * g : RADIX * (g + 1)] for value in natural], axis=0),
@@ -292,87 +332,123 @@
         high, low = parted(value)
         columns.append(jnp.concatenate([high, high, low], axis=0))
     profile = dot(fourth_ref[...], jnp.concatenate(columns, axis=1))
+
+    pairs = []
     for m in range(MS):
         re = profile[0:8, LANES * m : LANES * (m + 1)]
         im = profile[8:16, LANES * m : LANES * (m + 1)]
-        send_ref[0, pl.ds(m, 8, stride=8), :] = jnp.where(lane8 < 64, re, pltpu.roll(im, 64, 1))
-        send_ref[1, pl.ds(m, 8, stride=8), :] = jnp.where(lane8 < 64, pltpu.roll(re, 64, 1), im)
-
-    pl.semaphore_wait(ready_sem, SYM - 1)
-    slot = pl.ds(pl.multiple_of(8 * (SYM * sub + sym), 8), 8)
-
-    def block(to_sub):
-        return send_ref.at[lax.rem(to_sub, 2), pl.ds(pl.multiple_of(8 * (to_sub // 2), 8), 8)]
-
+        pairs.append(
+            (
+                jnp.where(lane8 < 64, re, pltpu.roll(im, 64, 1)),
+                jnp.where(lane8 < 64, pltpu.roll(re, 64, 1), im),
+            )
+        )
+    for half in range(2):
+        largest = functools.reduce(jnp.maximum, [jnp.abs(pair[half]) for pair in pairs])
+        largest = jnp.maximum(jnp.max(largest, axis=1, keepdims=True), 1e-30)
+        code = jnp.broadcast_to(jnp.ceil(jnp.log2(largest) * 256.0), (8, LANES))
+        inverse = 32767.0 * jnp.exp2(code * (-1.0 / 256.0))
+        for m in range(MS):
+            value = jnp.clip(jnp.round(pairs[m][half] * inverse), -32767.0, 32767.0)
+            stage_ref[half, pl.ds(m, 8, stride=8), :] = value.astype(jnp.int32)
+        stage_ref[half, pl.ds(MS, 8, stride=8), :] = code.astype(jnp.int32)
+        stage_ref[half, pl.ds(MS + 1, 8, stride=8), :] = jnp.zeros((8, LANES), jnp.int32)
+        for u in range(8):
+            send_ref[2 * u + half] = stage_ref[half, pl.ds(8 * u, 8), :].astype(jnp.int16)
+
+    pl.semaphore_wait(far_sem, 1)
+    slot = SUB * sym + sub
     for e in (2, 1, 3, 0):
-        for d in range(SUB):
+        for d in (8, 9, 10, 11, 7, 6, 5, 4, 12, 13, 14, 15, 3, 2, 1, 0):
             if e == 0 and d == 0:
                 continue
             to_sub = lax.rem(sub + d, SUB)
             pltpu.make_async_remote_copy(
-                src_ref=block(to_sub),
+                src_ref=send_ref.at[to_sub],
                 dst_ref=recv_ref.at[slot],
                 send_sem=send_sem,
                 recv_sem=recv_sem,
                 device_id={"sym": lax.rem(sym + e, SYM), "sub": to_sub},
                 device_id_type=MESH,
             ).start()
-    recv_ref[slot, :] = send_ref[lax.rem(sub, 2), pl.ds(pl.multiple_of(8 * (sub // 2), 8), 8), :]
-
-    everything = recv_ref.at[pl.ds(0, 8 * (SYM * SUB - 1))]
-    pltpu.make_async_remote_copy(
+    recv_ref[slot] = send_ref[sub]
+
+    everything = recv_ref.at[pl.ds(0, SYM * SUB - 1)]
+    copies = pltpu.make_async_remote_copy(
         src_ref=everything,
         dst_ref=everything,
         send_sem=send_sem,
         recv_sem=recv_sem,
         device_id={"sub": lax.rem(sub + 1, SUB)},
         device_id_type=MESH,
-    ).wait()
-
-    columns = []
-    for c in range(SUB):
-        value = recv_ref[pl.ds(32 * c, 32), :]
-        turned = pltpu.roll(value, 64, 1)
-        turned = jnp.where(lane < 64, turned, -turned)
-        high, low = parted(jnp.concatenate([value, turned], axis=0))
-        columns.append(jnp.concatenate([high, high, low], axis=0))
-    result = dot(doppler_ref[sym], jnp.concatenate(columns, axis=1))
-    for c in range(SUB):
-        value = result[0:8, LANES * c : LANES * (c + 1)]
-        out_ref[0, c, :, :] = value[0:MS, 0:64]
-        out_ref[1, c, :, :] = pltpu.roll(value, 64, 1)[0:MS, 0:64]
+    )
+    copies.wait_recv()
+    for i in range(SYM * SUB):
+        got_ref[pl.ds(8 * i, 8), :] = recv_ref[i].astype(jnp.int32).astype(F32)
+
+    cosines = [None] * MS
+    sines = [None] * MS
+    for s in range(SYM):
+        base = 8 * SUB * s
+        code = got_ref[pl.ds(base + MS, SUB, stride=8), :]
+        scale = jnp.exp2(code * (1.0 / 256.0)) * (1.0 / 32767.0)
+        for m in range(MS):
+            value = got_ref[pl.ds(base + m, SUB, stride=8), :] * scale
+            for f in range(MS):
+                at = SYMBOLS * f + MS * s + m
+                c = value * doppler_ref[0, at]
+                n = value * doppler_ref[0, SYMBOLS * MS + at]
+                cosines[f] = c if cosines[f] is None else cosines[f] + c
+                sines[f] = n if sines[f] is None else sines[f] + n
+    lane16 = lax.broadcasted_iota(jnp.int32, (SUB, LANES), 1)
+    for f in range(MS):
+        turned = pltpu.roll(sines[f], 64, 1)
+        value = cosines[f] + jnp.where(lane16 < 64, turned, -turned)
+        out_ref[0, f, :, :] = value[:, 0:64]
+        out_ref[1, f, :, :] = pltpu.roll(value, 64, 1)[:, 0:64]
+
+    index_copies.wait_send()
+    copies.wait_send()
 
 
 def body(samples, constellation_index, pilot_offsets, cp_offset):
     consts = [jnp.asarray(table) for table in tables()]
-    smem = pl.BlockSpec(memory_space=pltpu.SMEM)
     vmem = pl.BlockSpec(memory_space=pltpu.VMEM)
     hbm = pl.BlockSpec(memory_space=pl.ANY)
-    return pl.pallas_call(
+    records = samples.reshape(2 * MS * RECORD, LANES)
+    doppler = consts[-1]
+    out = pl.pallas_call(
         kernel,
-        out_shape=jax.ShapeDtypeStruct((2, SUB, MS, GUARD // SUB), F32),
-        in_specs=[smem, smem, hbm] + [vmem] * (1 + len(consts)),
+        out_shape=jax.ShapeDtypeStruct((2, MS, SUB, GUARD // SUB), F32),
+        in_specs=[hbm] * (4 + len(consts)),
         out_specs=vmem,
         scratch_shapes=[
-            pltpu.VMEM((2, MS, LENGTH + GUARD), F32),
-            pltpu.VMEM((2, 64 * MS, LANES), F32),
+            pltpu.SMEM((MS,), jnp.int32),
+            pltpu.SMEM((MS,), jnp.int32),
+            pltpu.VMEM(records.shape, F32),
+            pltpu.VMEM(constellation_index.shape, jnp.int32),
+            *[pltpu.VMEM(table.shape, table.dtype) for table in consts[:-1]],
+            pltpu.SMEM((1, doppler.shape[1]), F32),
             pltpu.VMEM((RADIX * MS, 512), BF16),
             pltpu.VMEM((RADIX * MS, 512), BF16),
-            pltpu.VMEM((16, LANES), F32),
-            pltpu.VMEM((16, LANES), BF16),
-            pltpu.VMEM((16 * SUB, LANES), BF16),
+            pltpu.VMEM((2 * MS, LANES), BF16),
+            pltpu.VMEM((SUB, 2 * MS, LANES), BF16),
             pltpu.VMEM((16 * SUB, LANES), F32),
-            pltpu.VMEM((2, 64, LANES), F32),
+            pltpu.VMEM((2, 64, LANES), jnp.int32),
+            pltpu.VMEM((SUB, 8, LANES), jnp.int16),
+            pltpu.VMEM((SYM * SUB, 8, LANES), jnp.int16),
             pltpu.VMEM((8 * SYM * SUB, LANES), F32),
-            pltpu.SemaphoreType.DMA,
+            pltpu.SemaphoreType.DMA((13,)),
             pltpu.SemaphoreType.DMA,
             pltpu.SemaphoreType.DMA,
             pltpu.SemaphoreType.DMA,
             pltpu.SemaphoreType.DMA,
             pltpu.SemaphoreType.REGULAR,
+            pltpu.SemaphoreType.REGULAR,
         ],
         compiler_params=pltpu.CompilerParams(collective_id=0, has_side_effects=True),
-    )(cp_offset, pilot_offsets, samples, constellation_index, *consts)
+    )(cp_offset, pilot_offsets, records, constellation_index, *consts)
+    return out.transpose(0, 2, 1, 3)
 
 
 def solution(mesh):

time: 29.6 us -> 23.3 us (0.79)
  Pallas kernels: 25.9 us -> 21.7 us
  local copies, waits for them, and re-layouts: 3.5 us -> 1.54 us
    pallas_call x1, Pallas kernels: 25.9 us -> 21.7 us  [body(): pl.pallas_call(kernel, out_shape=jax.ShapeDtypeStruct((2, MS, SUB, GUARD...]
    pallas_call x1 -> x0, local copies, waits for them, and re-layouts: 1.57 us -> none  [body(): pl.pallas_call(kernel, out_shape=jax.ShapeDtypeStruct((2, SUB, MS, GUARD...]
    unnamed x1, local copies, waits for them, and re-layouts: 1.93 us -> 1.54 us
where the time goes in v1:
time: 23.3 us; the launch traced here: 23.2 us
  Pallas kernels  21.7 us (93%)
  local copies, waits for them, and re-layouts  1.54 us (7%)
    pallas_call x1, Pallas kernels, body(): pl.pallas_call(kernel, out_shape=jax.ShapeDtypeStruct((2, MS, SUB, GUARD...  21.7 us
    unnamed x1, local copies, waits for them, and re-layouts  1.54 us

profile of v1, /device:TPU:1, one launch (start us, length us, event | category | flops | bytes accessed | tf_op | source)
XLA Modules:
  0.0 23.2 jit_solution(5649173594575423175)
XLA Ops:
  0.0 21.7 %shard_map.127 = f32[2,6,16,64]{3,2,1,0:T(8,128)} custom-call(s32[6]{0:T(128)} %cp_hbm.1, s32[6]{0:T(128)} %pilot_hbm.1, f32[864,128]{1,0:T(8,128)} %bitcast.2, s32[6,256]{1,0:T(8,128)} %index_hbm.1, bf16[64,192]{1,0:T(8,128)(2,1)} %constant.18.clone.first_hbm, f32[2,32,256]{2,1,0:T(8,128)} %constant.19.clone.twist_hbm, ...), custom_call_target="tpu_custom_call" | custom-call | tf_op jit(solution)/shard_map/pallas_call | solution.py:420
  21.7 1.5 %copy.15 = f32[2,16,6,64]{3,1,2,0:T(8,128)} copy(f32[2,16,6,64]{3,1,2,0:T(8,128)} %bitcast.3) | data formatting | bytes 98304

commit v2 on v1

--- a/solution.py
+++ b/solution.py
@@ -419,7 +419,7 @@
     doppler = consts[-1]
     out = pl.pallas_call(
         kernel,
-        out_shape=jax.ShapeDtypeStruct((2, MS, SUB, GUARD // SUB), F32),
+        out_shape=pltpu.VMEM((2, MS, SUB, GUARD // SUB), F32),
         in_specs=[hbm] * (4 + len(consts)),
         out_specs=vmem,
         scratch_shapes=[

time: 23.3 us -> 21.8 us (0.936)
  local copies, waits for them, and re-layouts: 1.54 us -> 0.64 us
  Pallas kernels: 21.7 us -> 21.1 us
    unnamed x1, local copies, waits for them, and re-layouts: 1.54 us -> 0.64 us
    pallas_call x1, Pallas kernels: 21.7 us -> 21.1 us  [body(): pl.pallas_call(kernel, out_shape=pltpu.VMEM((2, MS, SUB, GUARD // SUB), F...]
where the time goes in v2:
time: 21.8 us; the launch traced here: 21.7 us
  Pallas kernels  21.1 us (97%)
  local copies, waits for them, and re-layouts  0.64 us (3%)
    pallas_call x1, Pallas kernels, body(): pl.pallas_call(kernel, out_shape=pltpu.VMEM((2, MS, SUB, GUARD // SUB), F...  21.1 us
    unnamed x1, local copies, waits for them, and re-layouts  0.64 us

profile of v2, /device:TPU:1, one launch (start us, length us, event | category | flops | bytes accessed | tf_op | source)
XLA Modules:
  0.0 21.7 jit_solution(6813544783783507247)
XLA Ops:
  0.0 21.1 %shard_map.127 = f32[2,6,16,64]{3,2,1,0:T(8,128)S(1)} custom-call(s32[6]{0:T(128)} %cp_hbm.1, s32[6]{0:T(128)} %pilot_hbm.1, f32[864,128]{1,0:T(8,128)} %bitcast.3, s32[6,256]{1,0:T(8,128)} %index_hbm.1, bf16[64,192]{1,0:T(8,128)(2,1)} %constant.18.clone.first_hbm, f32[2,32,256]{2,1,0:T(8,128)} %constant.19.clone.twist_hbm, ...), custom_call_target="tpu_custom_call" | custom-call | tf_op jit(solution)/shard_map/pallas_call | solution.py:420
  21.1 0.6 %copy.15 = f32[2,16,6,64]{3,1,2,0:T(8,128)} copy(f32[2,16,6,64]{3,1,2,0:T(8,128)S(1)} %bitcast.2) | data formatting | bytes 98304

commit v3 on v2

--- a/solution.py
+++ b/solution.py
@@ -27,6 +27,7 @@
 MS = 6
 SYMBOLS = 24
 SHIFTS = (-2, -1, 0, 1, 2)
+FAR_FIRST = (10, 11, 8, 9, 6, 7, 14, 15, 4, 5, 12, 13, 2, 3, 1)
 
 
 def halves(matrix):
@@ -143,7 +144,7 @@
     barrier = pltpu.get_barrier_semaphore()
     before, after = lax.rem(sym + SYM - 1, SYM), lax.rem(sym + 1, SYM)
 
-    for d in range(1, SUB):
+    for d in FAR_FIRST:
         pl.semaphore_signal(
             barrier, inc=1, device_id={"sub": lax.rem(sub + d, SUB)}, device_id_type=MESH
         )
@@ -184,7 +185,7 @@
     isend_ref[...] = jnp.concatenate([index[:, :LANES], index[:, LANES:]], axis=0).astype(BF16)
 
     pl.semaphore_wait(barrier, SUB + 1)
-    for d in (8, 9, 10, 11, 7, 6, 5, 4, 12, 13, 14, 15, 3, 2, 1):
+    for d in FAR_FIRST:
         pltpu.make_async_remote_copy(
             src_ref=isend_ref,
             dst_ref=igath_ref.at[sub],
@@ -238,8 +239,42 @@
     zh = zh_ref[...]
     spectra = dot(zh, second_ref[0]) + dot(zl_ref[...], second_ref[0]) + dot(zh, second_ref[1])
 
+
     for i in range(6, 13):
         loads[i].wait()
+
+    def tapering(right, part):
+        tapered = dot(taper_ref[:, : right.shape[0]], right)
+        sums = []
+        for i in range(part):
+            total = None
+            for at, shift in enumerate(SHIFTS):
+                term = tapered[RADIX * at : RADIX * (at + 1), LANES * i : LANES * (i + 1)]
+                if shift:
+                    term = pltpu.roll(term, (-shift) % LANES, 1)
+                    inside = lane < LANES - shift if shift > 0 else lane >= -shift
+                    term = jnp.where(inside, term, 0.0)
+                total = term if total is None else total + term
+            sums.append(total)
+        return sums
+
+    turned = []
+    pilots = []
+    for m in range(MS):
+        rows = slice(RADIX * m, RADIX * (m + 1))
+        lc = lane_cos[m : m + 1, :]
+        ls = lane_sin[m : m + 1, :]
+        rc = jnp.broadcast_to(row_cos[:, m : m + 1], (RADIX, LANES))
+        rs = jnp.broadcast_to(row_sin[:, m : m + 1], (RADIX, LANES))
+        phase_re = lc * rc - ls * rs
+        phase_im = lc * rs + ls * rc
+        re, im = spectra[rows, :LANES], spectra[rows, LANES:]
+        turned.append((re * phase_re - im * phase_im, re * phase_im + im * phase_re))
+        pilots.append(residue == pilot_ref[m])
+    inverses = []
+    for m in range(0, MS, 2):
+        right = jnp.concatenate([pilots[m].astype(BF16), pilots[m + 1].astype(BF16)], axis=1)
+        inverses += [1.0 / total for total in tapering(right, 2)]
     pl.semaphore_wait(near_sem, 2)
     pl.semaphore_signal(far_sem, inc=1, device_id={"sym": before}, device_id_type=MESH)
 
@@ -277,42 +312,17 @@
         level_re = 2.0 * (index[rows] - 8.0 * quadrature) - 7.0
         level_im = 2.0 * quadrature - 7.0
         factor = math.sqrt(42.0) / (level_re * level_re + level_im * level_im)
-        lc = lane_cos[m : m + 1, :]
-        ls = lane_sin[m : m + 1, :]
-        rc = jnp.broadcast_to(row_cos[:, m : m + 1], (RADIX, LANES))
-        rs = jnp.broadcast_to(row_sin[:, m : m + 1], (RADIX, LANES))
-        phase_re = (lc * rc - ls * rs) * factor
-        phase_im = (lc * rs + ls * rc) * factor
-        gain_re = phase_re * level_re + phase_im * level_im
-        gain_im = phase_im * level_re - phase_re * level_im
-        re, im = spectra[rows, :LANES], spectra[rows, LANES:]
-        ratio_re = re * gain_re - im * gain_im
-        ratio_im = re * gain_im + im * gain_re
-        ratio = jnp.concatenate([ratio_re, ratio_im], axis=1)
-        pilot = (residue == pilot_ref[m]).astype(F32)
-        high, low = parted(ratio * jnp.concatenate([pilot, pilot], axis=1))
-        right = jnp.concatenate(
-            [
-                jnp.concatenate([high, pilot.astype(BF16)], axis=1),
-                jnp.concatenate([low, jnp.zeros((RADIX, LANES), BF16)], axis=1),
-            ],
-            axis=0,
-        )
-        tapered = dot(taper_ref[...], right)
-        sums = []
-        for part in range(3):
-            total = None
-            for i, shift in enumerate(SHIFTS):
-                term = tapered[RADIX * i : RADIX * (i + 1), LANES * part : LANES * (part + 1)]
-                if shift:
-                    term = pltpu.roll(term, (-shift) % LANES, 1)
-                    inside = lane < LANES - shift if shift > 0 else lane >= -shift
-                    term = jnp.where(inside, term, 0.0)
-                total = term if total is None else total + term
-            sums.append(total)
-        inverse = 1.0 / sums[2]
+        scaled_re, scaled_im = level_re * factor, level_im * factor
+        re, im = turned[m]
+        ratio_re = re * scaled_re + im * scaled_im
+        ratio_im = im * scaled_re - re * scaled_im
+        picked = jnp.concatenate(
+            [jnp.where(pilots[m], ratio_re, 0.0), jnp.where(pilots[m], ratio_im, 0.0)], axis=1
+        )
+        high, low = parted(picked)
+        sums = tapering(jnp.concatenate([high, low], axis=0), 2)
         cleaned = jnp.concatenate(
-            [ratio_re - sums[0] * inverse, ratio_im - sums[1] * inverse], axis=1
+            [ratio_re - sums[0] * inverses[m], ratio_im - sums[1] * inverses[m]], axis=1
         )
         high, low = parted(cleaned)
         high_rows.append(high)
@@ -359,7 +369,7 @@
     pl.semaphore_wait(far_sem, 1)
     slot = SUB * sym + sub
     for e in (2, 1, 3, 0):
-        for d in (8, 9, 10, 11, 7, 6, 5, 4, 12, 13, 14, 15, 3, 2, 1, 0):
+        for d in (8, 9, 10, 11, 4, 5, 6, 7, 12, 13, 14, 15, 2, 3, 1, 0):
             if e == 0 and d == 0:
                 continue
             to_sub = lax.rem(sub + d, SUB)
@@ -367,35 +377,37 @@
                 src_ref=send_ref.at[to_sub],
                 dst_ref=recv_ref.at[slot],
                 send_sem=send_sem,
-                recv_sem=recv_sem,
+                recv_sem=recv_sem.at[e],
                 device_id={"sym": lax.rem(sym + e, SYM), "sub": to_sub},
                 device_id_type=MESH,
             ).start()
     recv_ref[slot] = send_ref[sub]
 
-    everything = recv_ref.at[pl.ds(0, SYM * SUB - 1)]
-    copies = pltpu.make_async_remote_copy(
-        src_ref=everything,
-        dst_ref=everything,
-        send_sem=send_sem,
-        recv_sem=recv_sem,
-        device_id={"sub": lax.rem(sub + 1, SUB)},
-        device_id_type=MESH,
-    )
-    copies.wait_recv()
-    for i in range(SYM * SUB):
-        got_ref[pl.ds(8 * i, 8), :] = recv_ref[i].astype(jnp.int32).astype(F32)
-
     cosines = [None] * MS
     sines = [None] * MS
-    for s in range(SYM):
-        base = 8 * SUB * s
+    for e in (0, 1, 3, 2):
+        count = SUB - 1 if e == 0 else SUB
+        some = recv_ref.at[pl.ds(0, count)]
+        pltpu.make_async_remote_copy(
+            src_ref=some,
+            dst_ref=some,
+            send_sem=send_sem,
+            recv_sem=recv_sem.at[e],
+            device_id={"sub": lax.rem(sub + 1, SUB)},
+            device_id_type=MESH,
+        ).wait_recv()
+        source = lax.rem(sym + SYM - e, SYM)
+        base = 8 * SUB * e
+        for i in range(SUB):
+            got_ref[pl.ds(base + 8 * i, 8), :] = (
+                recv_ref[SUB * source + i].astype(jnp.int32).astype(F32)
+            )
         code = got_ref[pl.ds(base + MS, SUB, stride=8), :]
         scale = jnp.exp2(code * (1.0 / 256.0)) * (1.0 / 32767.0)
         for m in range(MS):
             value = got_ref[pl.ds(base + m, SUB, stride=8), :] * scale
             for f in range(MS):
-                at = SYMBOLS * f + MS * s + m
+                at = SYMBOLS * f + MS * source + m
                 c = value * doppler_ref[0, at]
                 n = value * doppler_ref[0, SYMBOLS * MS + at]
                 cosines[f] = c if cosines[f] is None else cosines[f] + c
@@ -408,7 +420,15 @@
         out_ref[1, f, :, :] = pltpu.roll(value, 64, 1)[:, 0:64]
 
     index_copies.wait_send()
-    copies.wait_send()
+    everything = recv_ref.at[pl.ds(0, SYM * SUB - 1)]
+    pltpu.make_async_remote_copy(
+        src_ref=everything,
+        dst_ref=everything,
+        send_sem=send_sem,
+        recv_sem=recv_sem.at[0],
+        device_id={"sub": lax.rem(sub + 1, SUB)},
+        device_id_type=MESH,
+    ).wait_send()
 
 
 def body(samples, constellation_index, pilot_offsets, cp_offset):
@@ -442,7 +462,7 @@
             pltpu.SemaphoreType.DMA,
             pltpu.SemaphoreType.DMA,
             pltpu.SemaphoreType.DMA,
-            pltpu.SemaphoreType.DMA,
+            pltpu.SemaphoreType.DMA((SYM,)),
             pltpu.SemaphoreType.REGULAR,
             pltpu.SemaphoreType.REGULAR,
         ],

time: 21.8 us -> 21.6 us (level)
  no operation moved by 1% of the time
where the time goes in v3:
time: 21.6 us; the launch traced here: 21.5 us
  Pallas kernels  20.9 us (97%)
  local copies, waits for them, and re-layouts  0.64 us (3%)
    pallas_call x1, Pallas kernels, body(): pl.pallas_call(kernel, out_shape=pltpu.VMEM((2, MS, SUB, GUARD // SUB), F...  20.9 us
    unnamed x1, local copies, waits for them, and re-layouts  0.64 us

profile of v3, /device:TPU:1, one launch (start us, length us, event | category | flops | bytes accessed | tf_op | source)
XLA Modules:
  0.0 21.5 jit_solution(3273797135544087004)
XLA Ops:
  0.0 20.9 %shard_map.127 = f32[2,6,16,64]{3,2,1,0:T(8,128)S(1)} custom-call(s32[6]{0:T(128)} %cp_hbm.1, s32[6]{0:T(128)} %pilot_hbm.1, f32[864,128]{1,0:T(8,128)} %bitcast.3, s32[6,256]{1,0:T(8,128)} %index_hbm.1, bf16[64,192]{1,0:T(8,128)(2,1)} %constant.18.clone.first_hbm, f32[2,32,256]{2,1,0:T(8,128)} %constant.19.clone.twist_hbm, ...), custom_call_target="tpu_custom_call" | custom-call | tf_op jit(solution)/shard_map/pallas_call | solution.py:440
  20.9 0.6 %copy.15 = f32[2,16,6,64]{3,1,2,0:T(8,128)} copy(f32[2,16,6,64]{3,1,2,0:T(8,128)S(1)} %bitcast.2) | data formatting | bytes 98304

commit v4 on v3

--- a/solution.py
+++ b/solution.py
@@ -25,8 +25,9 @@
 SYM = 4
 SUB = 16
 MS = 6
+HS = 3
 SYMBOLS = 24
-SHIFTS = (-2, -1, 0, 1, 2)
+SHIFTS = ((0, 0, 32), (-1, 0, 32), (1, 0, 32), (-2, 0, 16), (2, 16, 32))
 FAR_FIRST = (10, 11, 8, 9, 6, 7, 14, 15, 4, 5, 12, 13, 2, 3, 1)
 
 
@@ -51,8 +52,8 @@
     c, s = np.cos(angle), np.sin(angle)
     second = np.stack(halves(np.block([[c, -s], [s, c]]) / math.sqrt(LENGTH)))
     rows = []
-    for shift in SHIFTS:
-        gap = RADIX * shift + p[None, :] - p[:, None]
+    for shift, low, high in SHIFTS:
+        gap = RADIX * shift + p[None, :] - p[low:high, None]
         rows.append(np.maximum(HALFSPAN + 1 - np.abs(gap), 0))
     taper = np.concatenate(rows, axis=0)
     taper = np.concatenate([taper, taper], axis=1).astype(ml_dtypes.bfloat16)
@@ -132,6 +133,7 @@
     recv_ref,
     got_ref,
     load_sem,
+    swap_sem,
     isend_sem,
     irecv_sem,
     send_sem,
@@ -143,6 +145,8 @@
     sub = lax.axis_index("sub")
     barrier = pltpu.get_barrier_semaphore()
     before, after = lax.rem(sym + SYM - 1, SYM), lax.rem(sym + 1, SYM)
+    core, pair = lax.rem(sub, 2), sub // 2
+    other = 1 - core
 
     for d in FAR_FIRST:
         pl.semaphore_signal(
@@ -150,6 +154,12 @@
         )
     for to in (before, after):
         pl.semaphore_signal(barrier, inc=1, device_id={"sym": to}, device_id_type=MESH)
+
+    def records(part, taker):
+        return pl.ds(pl.multiple_of(RECORD * (MS * part + HS * taker), 8), RECORD * HS)
+
+    def places(channel, part):
+        return pl.ds(pl.multiple_of(RECORD * HS * (2 * channel + part), 8), RECORD * HS)
 
     loads = [
         pltpu.make_async_copy(source, target, load_sem.at[i])
@@ -157,7 +167,6 @@
             (
                 (index_hbm, index_ref),
                 (cp_hbm, cp_ref),
-                (x_hbm, x_ref),
                 (first_hbm, first_ref),
                 (twist_hbm, twist_ref),
                 (second_hbm, second_ref),
@@ -171,6 +180,12 @@
             )
         )
     ]
+    for part in range(2):
+        loads.append(
+            pltpu.make_async_copy(
+                x_hbm.at[records(part, core)], x_ref.at[places(core, part)], load_sem.at[12 + part]
+            )
+        )
     for load in loads:
         load.start()
 
@@ -182,12 +197,16 @@
 
     loads[0].wait()
     index = index_ref[...].astype(F32)
-    isend_ref[...] = jnp.concatenate([index[:, :LANES], index[:, LANES:]], axis=0).astype(BF16)
+    for taker in range(2):
+        rows = slice(HS * taker, HS * (taker + 1))
+        isend_ref[taker] = jnp.concatenate(
+            [index[rows, :LANES], index[rows, LANES:]], axis=0
+        ).astype(BF16)
 
     pl.semaphore_wait(barrier, SUB + 1)
     for d in FAR_FIRST:
         pltpu.make_async_remote_copy(
-            src_ref=isend_ref,
+            src_ref=isend_ref.at[lax.rem(sub + d, 2)],
             dst_ref=igath_ref.at[sub],
             send_sem=isend_sem,
             recv_sem=irecv_sem,
@@ -196,85 +215,111 @@
         ).start()
     for to in (before, after):
         pl.semaphore_signal(near_sem, inc=1, device_id={"sym": to}, device_id_type=MESH)
-    igath_ref[sub] = isend_ref[...]
+    igath_ref[sub] = isend_ref[core]
+    swaps = []
+    for part in range(2):
+        swaps.append(
+            pltpu.make_async_remote_copy(
+                src_ref=x_hbm.at[records(part, other)],
+                dst_ref=x_ref.at[places(core, part)],
+                send_sem=swap_sem.at[part],
+                recv_sem=swap_sem.at[2 + part],
+                device_id={"sub": sub + 1 - 2 * core},
+                device_id_type=MESH,
+            )
+        )
+        swaps[part].start()
 
     loads[1].wait()
     start_lanes = jnp.zeros((RADIX, LANES), jnp.int32)
     start_rows = jnp.zeros((8, LANES), jnp.int32)
-    for m in range(MS):
-        start_lanes = jnp.where(lane == m, cp_ref[m], start_lanes)
-        start_rows = jnp.where(row8 == m, cp_ref[m], start_rows)
+    starts = [cp_ref[HS * core + i] for i in range(HS)]
+    for i in range(HS):
+        start_lanes = jnp.where(lane == i, starts[i], start_lanes)
+        start_rows = jnp.where(row8 == i, starts[i], start_rows)
     step = 2.0 * math.pi / LENGTH
     angle = ((start_lanes * row) & (LENGTH - 1)).astype(F32) * step
     row_cos, row_sin = jnp.cos(angle), jnp.sin(angle)
     angle = ((start_rows * (LOWEST + RADIX * lane8)) & (LENGTH - 1)).astype(F32) * step
     lane_cos, lane_sin = jnp.cos(angle), jnp.sin(angle)
 
-    for i in (2, 3, 4):
+    for i in (2, 3, 12, 13):
         loads[i].wait()
     place = LANES * row8 + lane8
     twist_cos, twist_sin = twist_ref[0], twist_ref[1]
-    for m in range(MS):
-        pieces = []
-        for part in range(2):
-            base = RECORD * (MS * part + m)
-            x_ref[pl.ds(base, 8), :] = jnp.where(
-                place >= cp_ref[m], x_ref[pl.ds(base, 8), :], x_ref[pl.ds(base + 64, 8), :]
-            )
-            pieces.append(
-                jnp.concatenate(
-                    [x_ref[pl.ds(base + i, RADIX, stride=2), :] for i in range(2)], axis=1
+    for turn, channel in enumerate((core, other)):
+        if turn:
+            for swap in swaps:
+                swap.wait_recv()
+        for i in range(HS):
+            pieces = []
+            for part in range(2):
+                base = pl.multiple_of(RECORD * (HS * (2 * channel + part) + i), 8)
+                x_ref[pl.ds(base, 8), :] = jnp.where(
+                    place >= starts[i], x_ref[pl.ds(base, 8), :], x_ref[pl.ds(base + 64, 8), :]
                 )
-            )
-        high, low = parted(jnp.concatenate(pieces, axis=0))
-        y = dot(first_ref[...], jnp.concatenate([high, high, low], axis=0))
-        re, im = y[:RADIX], y[RADIX:]
-        z = jnp.concatenate(
-            [re * twist_cos + im * twist_sin, im * twist_cos - re * twist_sin], axis=1
-        )
-        high, low = parted(z)
-        zh_ref[pl.ds(RADIX * m, RADIX), :] = high
-        zl_ref[pl.ds(RADIX * m, RADIX), :] = low
-    loads[5].wait()
+                pieces.append(
+                    jnp.concatenate(
+                        [x_ref[pl.ds(base + n, RADIX, stride=2), :] for n in range(2)], axis=1
+                    )
+                )
+            high, low = parted(jnp.concatenate(pieces, axis=0))
+            y = dot(first_ref[...], jnp.concatenate([high, high, low], axis=0))
+            re, im = y[:RADIX], y[RADIX:]
+            z = jnp.concatenate(
+                [re * twist_cos + im * twist_sin, im * twist_cos - re * twist_sin], axis=1
+            )
+            high, low = parted(z)
+            rows = pl.ds(pl.multiple_of(RADIX * (HS * channel + i), RADIX), RADIX)
+            zh_ref[rows, :] = high
+            zl_ref[rows, :] = low
+    loads[4].wait()
     zh = zh_ref[...]
     spectra = dot(zh, second_ref[0]) + dot(zl_ref[...], second_ref[0]) + dot(zh, second_ref[1])
 
 
-    for i in range(6, 13):
+    for i in range(5, 12):
         loads[i].wait()
 
-    def tapering(right, part):
+    def tapering(right, count):
         tapered = dot(taper_ref[:, : right.shape[0]], right)
         sums = []
-        for i in range(part):
-            total = None
-            for at, shift in enumerate(SHIFTS):
-                term = tapered[RADIX * at : RADIX * (at + 1), LANES * i : LANES * (i + 1)]
+        for n in range(count):
+            halves_of = [None, None]
+            at = 0
+            for shift, low, high in SHIFTS:
+                term = tapered[at : at + high - low, LANES * n : LANES * (n + 1)]
+                at += high - low
                 if shift:
                     term = pltpu.roll(term, (-shift) % LANES, 1)
-                    inside = lane < LANES - shift if shift > 0 else lane >= -shift
+                    inside = lane[low:high] < LANES - shift if shift > 0 else lane[low:high] >= -shift
                     term = jnp.where(inside, term, 0.0)
-                total = term if total is None else total + term
-            sums.append(total)
+                for half in range(2):
+                    if low <= 16 * half < high:
+                        piece = term[16 * half - low : 16 * half - low + 16]
+                        halves_of[half] = (
+                            piece if halves_of[half] is None else halves_of[half] + piece
+                        )
+            sums.append(jnp.concatenate(halves_of, axis=0))
         return sums
 
-    turned = []
+    turned = [None] * MS
     pilots = []
-    for m in range(MS):
-        rows = slice(RADIX * m, RADIX * (m + 1))
-        lc = lane_cos[m : m + 1, :]
-        ls = lane_sin[m : m + 1, :]
-        rc = jnp.broadcast_to(row_cos[:, m : m + 1], (RADIX, LANES))
-        rs = jnp.broadcast_to(row_sin[:, m : m + 1], (RADIX, LANES))
+    for i in range(HS):
+        lc = lane_cos[i : i + 1, :]
+        ls = lane_sin[i : i + 1, :]
+        rc = jnp.broadcast_to(row_cos[:, i : i + 1], (RADIX, LANES))
+        rs = jnp.broadcast_to(row_sin[:, i : i + 1], (RADIX, LANES))
         phase_re = lc * rc - ls * rs
         phase_im = lc * rs + ls * rc
-        re, im = spectra[rows, :LANES], spectra[rows, LANES:]
-        turned.append((re * phase_re - im * phase_im, re * phase_im + im * phase_re))
-        pilots.append(residue == pilot_ref[m])
-    inverses = []
-    for m in range(0, MS, 2):
-        right = jnp.concatenate([pilots[m].astype(BF16), pilots[m + 1].astype(BF16)], axis=1)
-        inverses += [1.0 / total for total in tapering(right, 2)]
+        for channel in range(2):
+            m = HS * channel + i
+            rows = slice(RADIX * m, RADIX * (m + 1))
+            re, im = spectra[rows, :LANES], spectra[rows, LANES:]
+            turned[m] = (re * phase_re - im * phase_im, re * phase_im + im * phase_re)
+        pilots.append(residue == pilot_ref[HS * core + i])
+    right = jnp.concatenate([pilot.astype(BF16) for pilot in pilots], axis=1)
+    inverses = [1.0 / total for total in tapering(right, HS)]
     pl.semaphore_wait(near_sem, 2)
     pl.semaphore_signal(far_sem, inc=1, device_id={"sym": before}, device_id_type=MESH)
 
@@ -289,12 +334,12 @@
     )
     index_copies.wait_recv()
     for owner in range(SUB):
-        ig_ref[pl.ds(16 * owner, 2 * MS), :] = igath_ref[owner].astype(F32)
+        ig_ref[pl.ds(8 * owner, 2 * HS), :] = igath_ref[owner].astype(F32)
 
     natural = []
-    for m in range(MS):
+    for i in range(HS):
         value = jnp.concatenate(
-            [ig_ref[pl.ds(MS * half + m, SUB, stride=16), :] for half in range(2)], axis=0
+            [ig_ref[pl.ds(HS * half + i, SUB, stride=8), :] for half in range(2)], axis=0
         )
         natural.append(jnp.transpose(value).astype(BF16))
     index = sum(
@@ -305,28 +350,27 @@
         for g in range(4)
     )
 
-    high_rows, low_rows = [], []
-    for m in range(MS):
-        rows = slice(RADIX * m, RADIX * (m + 1))
-        quadrature = jnp.floor(index[rows] * 0.125)
-        level_re = 2.0 * (index[rows] - 8.0 * quadrature) - 7.0
+    high_rows, low_rows = [None] * MS, [None] * MS
+    for i in range(HS):
+        value = index[RADIX * i : RADIX * (i + 1)]
+        quadrature = jnp.floor(value * 0.125)
+        level_re = 2.0 * (value - 8.0 * quadrature) - 7.0
         level_im = 2.0 * quadrature - 7.0
         factor = math.sqrt(42.0) / (level_re * level_re + level_im * level_im)
         scaled_re, scaled_im = level_re * factor, level_im * factor
-        re, im = turned[m]
-        ratio_re = re * scaled_re + im * scaled_im
-        ratio_im = im * scaled_re - re * scaled_im
-        picked = jnp.concatenate(
-            [jnp.where(pilots[m], ratio_re, 0.0), jnp.where(pilots[m], ratio_im, 0.0)], axis=1
-        )
-        high, low = parted(picked)
-        sums = tapering(jnp.concatenate([high, low], axis=0), 2)
-        cleaned = jnp.concatenate(
-            [ratio_re - sums[0] * inverses[m], ratio_im - sums[1] * inverses[m]], axis=1
-        )
-        high, low = parted(cleaned)
-        high_rows.append(high)
-        low_rows.append(low)
+        for m in (i, HS + i):
+            re, im = turned[m]
+            ratio_re = re * scaled_re + im * scaled_im
+            ratio_im = im * scaled_re - re * scaled_im
+            picked = jnp.concatenate(
+                [jnp.where(pilots[i], ratio_re, 0.0), jnp.where(pilots[i], ratio_im, 0.0)], axis=1
+            )
+            high, low = parted(picked)
+            sums = tapering(jnp.concatenate([high, low], axis=0), 2)
+            cleaned = jnp.concatenate(
+                [ratio_re - sums[0] * inverses[i], ratio_im - sums[1] * inverses[i]], axis=1
+            )
+            high_rows[m], low_rows[m] = parted(cleaned)
     high = jnp.concatenate(high_rows, axis=0)
     low = jnp.concatenate(low_rows, axis=0)
     folded = dot(high, third_ref[0]) + dot(low, third_ref[0]) + dot(high, third_ref[1])
@@ -354,20 +398,21 @@
             )
         )
     for half in range(2):
-        largest = functools.reduce(jnp.maximum, [jnp.abs(pair[half]) for pair in pairs])
-        largest = jnp.maximum(jnp.max(largest, axis=1, keepdims=True), 1e-30)
-        code = jnp.broadcast_to(jnp.ceil(jnp.log2(largest) * 256.0), (8, LANES))
-        inverse = 32767.0 * jnp.exp2(code * (-1.0 / 256.0))
-        for m in range(MS):
-            value = jnp.clip(jnp.round(pairs[m][half] * inverse), -32767.0, 32767.0)
-            stage_ref[half, pl.ds(m, 8, stride=8), :] = value.astype(jnp.int32)
-        stage_ref[half, pl.ds(MS, 8, stride=8), :] = code.astype(jnp.int32)
-        stage_ref[half, pl.ds(MS + 1, 8, stride=8), :] = jnp.zeros((8, LANES), jnp.int32)
+        for channel in range(2):
+            some = [pairs[HS * channel + i][half] for i in range(HS)]
+            largest = functools.reduce(jnp.maximum, [jnp.abs(value) for value in some])
+            largest = jnp.maximum(jnp.max(largest, axis=1, keepdims=True), 1e-30)
+            code = jnp.broadcast_to(jnp.ceil(jnp.log2(largest) * 256.0), (8, LANES))
+            inverse = 32767.0 * jnp.exp2(code * (-1.0 / 256.0))
+            for i in range(HS):
+                value = jnp.clip(jnp.round(some[i] * inverse), -32767.0, 32767.0)
+                stage_ref[half, pl.ds(4 * channel + i, 8, stride=8), :] = value.astype(jnp.int32)
+            stage_ref[half, pl.ds(4 * channel + HS, 8, stride=8), :] = code.astype(jnp.int32)
         for u in range(8):
             send_ref[2 * u + half] = stage_ref[half, pl.ds(8 * u, 8), :].astype(jnp.int16)
 
     pl.semaphore_wait(far_sem, 1)
-    slot = SUB * sym + sub
+    slot = SUB * sym + 8 * core + pair
     for e in (2, 1, 3, 0):
         for d in (8, 9, 10, 11, 4, 5, 6, 7, 12, 13, 14, 15, 2, 3, 1, 0):
             if e == 0 and d == 0:
@@ -402,16 +447,18 @@
             got_ref[pl.ds(base + 8 * i, 8), :] = (
                 recv_ref[SUB * source + i].astype(jnp.int32).astype(F32)
             )
-        code = got_ref[pl.ds(base + MS, SUB, stride=8), :]
-        scale = jnp.exp2(code * (1.0 / 256.0)) * (1.0 / 32767.0)
-        for m in range(MS):
-            value = got_ref[pl.ds(base + m, SUB, stride=8), :] * scale
-            for f in range(MS):
-                at = SYMBOLS * f + MS * source + m
-                c = value * doppler_ref[0, at]
-                n = value * doppler_ref[0, SYMBOLS * MS + at]
-                cosines[f] = c if cosines[f] is None else cosines[f] + c
-                sines[f] = n if sines[f] is None else sines[f] + n
+        for taker in range(2):
+            first = base + 64 * taker
+            code = got_ref[pl.ds(first + HS, SUB, stride=4), :]
+            scale = jnp.exp2(code * (1.0 / 256.0)) * (1.0 / 32767.0)
+            for i in range(HS):
+                value = got_ref[pl.ds(first + i, SUB, stride=4), :] * scale
+                for f in range(MS):
+                    at = SYMBOLS * f + MS * source + HS * taker + i
+                    c = value * doppler_ref[0, at]
+                    n = value * doppler_ref[0, SYMBOLS * MS + at]
+                    cosines[f] = c if cosines[f] is None else cosines[f] + c
+                    sines[f] = n if sines[f] is None else sines[f] + n
     lane16 = lax.broadcasted_iota(jnp.int32, (SUB, LANES), 1)
     for f in range(MS):
         turned = pltpu.roll(sines[f], 64, 1)
@@ -420,6 +467,8 @@
         out_ref[1, f, :, :] = pltpu.roll(value, 64, 1)[:, 0:64]
 
     index_copies.wait_send()
+    for swap in swaps:
+        swap.wait_send()
     everything = recv_ref.at[pl.ds(0, SYM * SUB - 1)]
     pltpu.make_async_remote_copy(
         src_ref=everything,
@@ -445,20 +494,21 @@
         scratch_shapes=[
             pltpu.SMEM((MS,), jnp.int32),
             pltpu.SMEM((MS,), jnp.int32),
-            pltpu.VMEM(records.shape, F32),
+            pltpu.VMEM((4 * HS * RECORD, LANES), F32),
             pltpu.VMEM(constellation_index.shape, jnp.int32),
             *[pltpu.VMEM(table.shape, table.dtype) for table in consts[:-1]],
             pltpu.SMEM((1, doppler.shape[1]), F32),
             pltpu.VMEM((RADIX * MS, 512), BF16),
             pltpu.VMEM((RADIX * MS, 512), BF16),
-            pltpu.VMEM((2 * MS, LANES), BF16),
-            pltpu.VMEM((SUB, 2 * MS, LANES), BF16),
-            pltpu.VMEM((16 * SUB, LANES), F32),
+            pltpu.VMEM((2, 2 * HS, LANES), BF16),
+            pltpu.VMEM((SUB, 2 * HS, LANES), BF16),
+            pltpu.VMEM((8 * SUB, LANES), F32),
             pltpu.VMEM((2, 64, LANES), jnp.int32),
             pltpu.VMEM((SUB, 8, LANES), jnp.int16),
             pltpu.VMEM((SYM * SUB, 8, LANES), jnp.int16),
             pltpu.VMEM((8 * SYM * SUB, LANES), F32),
-            pltpu.SemaphoreType.DMA((13,)),
+            pltpu.SemaphoreType.DMA((14,)),
+            pltpu.SemaphoreType.DMA((4,)),
             pltpu.SemaphoreType.DMA,
             pltpu.SemaphoreType.DMA,
             pltpu.SemaphoreType.DMA,

time: 21.6 us -> 21.4 us (level)
  Pallas kernels: 20.9 us -> 20.6 us
    pallas_call x1, Pallas kernels: 20.9 us -> 20.6 us  [body(): pl.pallas_call(kernel, out_shape=pltpu.VMEM((2, MS, SUB, GUARD // SUB), F...]
where the time goes in v4:
time: 21.4 us; the launch traced here: 21.3 us
  Pallas kernels  20.6 us (96%)
  local copies, waits for them, and re-layouts  0.64 us (3%)
    pallas_call x1, Pallas kernels, body(): pl.pallas_call(kernel, out_shape=pltpu.VMEM((2, MS, SUB, GUARD // SUB), F...  20.6 us
    unnamed x1, local copies, waits for them, and re-layouts  0.64 us

profile of v4, /device:TPU:1, one launch (start us, length us, event | category | flops | bytes accessed | tf_op | source)
XLA Modules:
  0.0 21.3 jit_solution(5113925102165051190)
XLA Ops:
  0.0 20.6 %shard_map.127 = f32[2,6,16,64]{3,2,1,0:T(8,128)S(1)} custom-call(s32[6]{0:T(128)} %cp_hbm.1, s32[6]{0:T(128)} %pilot_hbm.1, f32[864,128]{1,0:T(8,128)} %bitcast.3, s32[6,256]{1,0:T(8,128)} %index_hbm.1, bf16[64,192]{1,0:T(8,128)(2,1)} %constant.18.clone.first_hbm, f32[2,32,256]{2,1,0:T(8,128)} %constant.19.clone.twist_hbm, ...), custom_call_target="tpu_custom_call" | custom-call | tf_op jit(solution)/shard_map/pallas_call | solution.py:489
  20.6 0.6 %copy.15 = f32[2,16,6,64]{3,1,2,0:T(8,128)} copy(f32[2,16,6,64]{3,1,2,0:T(8,128)S(1)} %bitcast.2) | data formatting | bytes 98304

commit v5 on v4

--- a/solution.py
+++ b/solution.py
@@ -28,7 +28,19 @@
 HS = 3
 SYMBOLS = 24
 SHIFTS = ((0, 0, 32), (-1, 0, 32), (1, 0, 32), (-2, 0, 16), (2, 16, 32))
-FAR_FIRST = (10, 11, 8, 9, 6, 7, 14, 15, 4, 5, 12, 13, 2, 3, 1)
+STEPS = [(y, z, c) for y in range(4) for z in range(2) for c in range(2)]
+FAR_FIRST = sorted(STEPS[1:], key=lambda step: -min(step[0], 4 - step[0]) - step[1] - 0.5 * step[2])
+
+
+def hops(move):
+    e, (y, z, c) = move
+    along = 4 - z if e == 2 else 2 if e else z
+    return min(y, 4 - y) + along + 0.5 * c
+
+
+EXCHANGE = sorted(
+    ((e, step) for e in range(SYM) for step in STEPS if e or any(step)), key=hops, reverse=True
+)
 
 
 def halves(matrix):
@@ -147,10 +159,18 @@
     before, after = lax.rem(sym + SYM - 1, SYM), lax.rem(sym + 1, SYM)
     core, pair = lax.rem(sub, 2), sub // 2
     other = 1 - core
-
-    for d in FAR_FIRST:
+    at_y = [4 * lax.rem(sub // 4 + y, 4) for y in range(4)]
+    at_z = [2 * lax.rem(sub // 2 + z, 2) for z in range(2)]
+    at_core = [core, other]
+
+    def stepped(step):
+        y, z, c = step
+        return at_y[y] + at_z[z] + at_core[c]
+
+
+    for step in FAR_FIRST:
         pl.semaphore_signal(
-            barrier, inc=1, device_id={"sub": lax.rem(sub + d, SUB)}, device_id_type=MESH
+            barrier, inc=1, device_id={"sub": stepped(step)}, device_id_type=MESH
         )
     for to in (before, after):
         pl.semaphore_signal(barrier, inc=1, device_id={"sym": to}, device_id_type=MESH)
@@ -204,13 +224,13 @@
         ).astype(BF16)
 
     pl.semaphore_wait(barrier, SUB + 1)
-    for d in FAR_FIRST:
+    for step in FAR_FIRST:
         pltpu.make_async_remote_copy(
-            src_ref=isend_ref.at[lax.rem(sub + d, 2)],
+            src_ref=isend_ref.at[at_core[step[2]]],
             dst_ref=igath_ref.at[sub],
             send_sem=isend_sem,
             recv_sem=irecv_sem,
-            device_id={"sub": lax.rem(sub + d, SUB)},
+            device_id={"sub": stepped(step)},
             device_id_type=MESH,
         ).start()
     for to in (before, after):
@@ -413,19 +433,16 @@
 
     pl.semaphore_wait(far_sem, 1)
     slot = SUB * sym + 8 * core + pair
-    for e in (2, 1, 3, 0):
-        for d in (8, 9, 10, 11, 4, 5, 6, 7, 12, 13, 14, 15, 2, 3, 1, 0):
-            if e == 0 and d == 0:
-                continue
-            to_sub = lax.rem(sub + d, SUB)
-            pltpu.make_async_remote_copy(
-                src_ref=send_ref.at[to_sub],
-                dst_ref=recv_ref.at[slot],
-                send_sem=send_sem,
-                recv_sem=recv_sem.at[e],
-                device_id={"sym": lax.rem(sym + e, SYM), "sub": to_sub},
-                device_id_type=MESH,
-            ).start()
+    for e, step in EXCHANGE:
+        to_sub = stepped(step)
+        pltpu.make_async_remote_copy(
+            src_ref=send_ref.at[to_sub],
+            dst_ref=recv_ref.at[slot],
+            send_sem=send_sem,
+            recv_sem=recv_sem.at[e],
+            device_id={"sym": lax.rem(sym + e, SYM), "sub": to_sub},
+            device_id_type=MESH,
+        ).start()
     recv_ref[slot] = send_ref[sub]
 
     cosines = [None] * MS

time: 21.4 us -> 21.1 us (0.986)
  Pallas kernels: 20.6 us -> 20.3 us
    pallas_call x1, Pallas kernels: 20.6 us -> 20.3 us  [body(): pl.pallas_call(kernel, out_shape=pltpu.VMEM((2, MS, SUB, GUARD // SUB), F...]
where the time goes in v5:
time: 21.1 us; the launch traced here: 21 us
  Pallas kernels  20.3 us (96%)
  local copies, waits for them, and re-layouts  0.64 us (3%)
    pallas_call x1, Pallas kernels, body(): pl.pallas_call(kernel, out_shape=pltpu.VMEM((2, MS, SUB, GUARD // SUB), F...  20.3 us
    unnamed x1, local copies, waits for them, and re-layouts  0.64 us

profile of v5, /device:TPU:1, one launch (start us, length us, event | category | flops | bytes accessed | tf_op | source)
XLA Modules:
  0.0 21.0 jit_solution(15988208242213518760)
XLA Ops:
  0.0 20.3 %shard_map.127 = f32[2,6,16,64]{3,2,1,0:T(8,128)S(1)} custom-call(s32[6]{0:T(128)} %cp_hbm.1, s32[6]{0:T(128)} %pilot_hbm.1, f32[864,128]{1,0:T(8,128)} %bitcast.3, s32[6,256]{1,0:T(8,128)} %index_hbm.1, bf16[64,192]{1,0:T(8,128)(2,1)} %constant.18.clone.first_hbm, f32[2,32,256]{2,1,0:T(8,128)} %constant.19.clone.twist_hbm, ...), custom_call_target="tpu_custom_call" | custom-call | tf_op jit(solution)/shard_map/pallas_call | solution.py:506
  20.3 0.6 %copy.15 = f32[2,16,6,64]{3,1,2,0:T(8,128)} copy(f32[2,16,6,64]{3,1,2,0:T(8,128)S(1)} %bitcast.2) | data formatting | bytes 98304
